TPU v7x, 32 devices: a whole 2x2x4 slice. The times are simulated.
32 devices in a mesh: gx: 8 (over y, x, core), gy: 4 (over z).
Axes of the slice: x: 2, y: 2, z: 4, core: 2. Of those that a mesh axis runs over, the one named last changes fastest.
Arguments:
- activations: bfloat16 [40960, 5120], P(('gx', 'gy')), may hold values from -6 to 6
- out_grad: bfloat16 [2, 40960, 32], P(None, ('gx', 'gy')), may hold values from -0.0390625 to 0.0390625
- master: float32 [32, 2, 5120], P(('gx', 'gy')), may hold values from -1 to 1
- first_moment: bfloat16 [32, 2, 5120], P(('gx', 'gy')), may hold values from -1 to 1
- first_scale: float32 [32, 2, 40], P(('gx', 'gy')), may hold values from 0.05 to 0.5
- second_moment: bfloat16 [32, 2, 5120], P(('gx', 'gy')), may hold values from 0.099609375 to 1
- second_scale: float32 [32, 2, 40], P(('gx', 'gy')), may hold values from 0.05 to 0.5
Outputs:
- new_weights: bfloat16 [32, 2, 5120], replicated
- new_master: float32 [32, 2, 5120], P(('gx', 'gy'))
- new_first: bfloat16 [32, 2, 5120], P(('gx', 'gy'))
- new_first_scale: float32 [32, 2, 40], P(('gx', 'gy'))
- new_second: bfloat16 [32, 2, 5120], P(('gx', 'gy'))
- new_second_scale: float32 [32, 2, 40], P(('gx', 'gy'))
All inputs are finite; a program needn't handle non-finite values. Where the computation divides by a largest or mean magnitude, that divisor is 1e-20 or more.
Results may differ from a plain program's by a relative error of at most 0.0014.
Values may be sent and summed in bfloat16 or wider, within the bound.
A program may use at most 128 MiB of HBM per device.

v0:
```python
import jax
import jax.numpy as jnp
from jax import lax
from jax.sharding import PartitionSpec as P

beta_one = 0.9
beta_two = 0.95
epsilon = 1e-08
learn_rate = 0.01
decay_rate = 0.1
step_count = 10


def expand(quant, scales):
    row_count, pair_count, width_all = quant.shape
    group_count = scales.shape[2]
    blocks = quant.astype(jnp.float32).reshape(
        row_count, pair_count, group_count, width_all // group_count
    )
    return (blocks * scales[..., None]).reshape(row_count, pair_count, width_all)


def requant(values, group_count):
    row_count, pair_count, width_all = values.shape
    blocks = values.reshape(row_count, pair_count, group_count, width_all // group_count)
    scales = jnp.max(jnp.abs(blocks), axis=3) + 1e-06
    quant = (
        (blocks / scales[..., None]).reshape(row_count, pair_count, width_all).astype(jnp.bfloat16)
    )
    return (quant, scales)


def adam_owned(gradient, master, first_moment, first_scale, second_moment, second_scale):
    group_count = first_scale.shape[2]
    first_old = expand(first_moment, first_scale)
    second_old = expand(second_moment, second_scale)
    first_new = beta_one * first_old + (1.0 - beta_one) * gradient
    second_new = beta_two * second_old + (1.0 - beta_two) * gradient * gradient
    correct_one = 1.0 - beta_one**step_count
    correct_two = 1.0 - beta_two**step_count
    update = first_new / correct_one / (jnp.sqrt(second_new / correct_two) + epsilon)
    new_master = master - learn_rate * (update + decay_rate * master)
    new_first, new_first_scale = requant(first_new, group_count)
    new_second, new_second_scale = requant(second_new, group_count)
    return (new_master, new_first, new_first_scale, new_second, new_second_scale)


def body(activations, out_grad, master, first_moment, first_scale, second_moment, second_scale):
    partial_rows = lax.psum_scatter(
        jnp.einsum("ptr,td->rpd", out_grad, activations, preferred_element_type=jnp.float32),
        "gx",
        scatter_dimension=0,
        tiled=True,
    )
    gradient = lax.psum_scatter(partial_rows, "gy", scatter_dimension=0, tiled=True)
    new_master, new_first, new_first_scale, new_second, new_second_scale = adam_owned(
        gradient, master, first_moment, first_scale, second_moment, second_scale
    )
    local_weights = new_master.astype(jnp.bfloat16)
    inner_weights = lax.all_gather(local_weights, "gy", axis=0, tiled=True)
    new_weights = lax.all_gather(inner_weights, "gx", axis=0, tiled=True)
    return (new_weights, new_master, new_first, new_first_scale, new_second, new_second_scale)


def solution(mesh):
    in_specs = (
        P(("gx", "gy"), None),
        P(None, ("gx", "gy"), None),
        P(("gx", "gy"), None, None),
        P(("gx", "gy"), None, None),
        P(("gx", "gy"), None, None),
        P(("gx", "gy"), None, None),
        P(("gx", "gy"), None, None),
    )
    out_specs = (
        P(),
        P(("gx", "gy"), None, None),
        P(("gx", "gy"), None, None),
        P(("gx", "gy"), None, None),
        P(("gx", "gy"), None, None),
        P(("gx", "gy"), None, None),
    )
    return jax.shard_map(body, mesh=mesh, in_specs=in_specs, out_specs=out_specs, check_vma=False)
```

profile of v0, /device:TPU:0, one launch (start us, length us, event | category | flops | bytes accessed | tf_op | source)
XLA Modules:
  0.0 148.4 jit_solution(13711330916889499568)
XLA Ops:
  7.3 0.0 all-reduce.5.cloned.1.call-start
  7.3 0.8 copy-done
  8.1 8.2 %fusion.5 = f32[5120,64]{0,1} fusion(bf16[1280,64]{0,1:T(8,128)(2,1)S(1)} %bitcast.26, bf16[1280,5120]{1,0:T(8,128)(2,1)} %param.7), kind=kOutput, calls=%fused_computation.16 | convolution fusion | flops 838860800 | bytes 14581760
  16.3 0.0 all-reduce.5.cloned.1.call-update
  16.3 0.0 all-reduce.7.cloned.1.call-start
  16.4 0.6 dynamic-slice
  17.6 59.3 %all-reduce.5.cloned.1.call-done = f32[32,2,5120]{2,0,1:T(8,128)} async-done(((f32[32,2,5120]{2,0,1:T(8,128)}), f32[32,2,5120]{2,0,1:T(8,128)}) %all-reduce.5.cloned.1.call-update) | async-done | bytes 1310736
  76.9 1.0 constant_dynamic-slice_fusion
  77.9 0.8 copy.22
  78.7 0.0 all-reduce.7.cloned.1.call-update
  78.8 0.6 dynamic-slice.2
  79.4 0.1 mul.70
  79.5 0.1 mul.77
  79.6 34.2 %all-reduce.7.cloned.1.call-done = f32[4,2,5120]{2,1,0:T(2,128)} async-done(((f32[4,2,5120]{2,1,0:T(2,128)}), f32[4,2,5120]{2,1,0:T(2,128)}) %all-reduce.7.cloned.1.call-update) | async-done | bytes 163856
  113.8 1.5 %abs_bitcast_fusion.1 = (f32[1,2,40,128]{3,1,2,0:T(2,128)S(1)}, f32[1,2,5120]{2,1,0:T(2,128)S(1)}, f32[1,2,40,128]{3,1,2,0:T(2,128)S(1)}, f32[1,2,5120]{2,1,0:T(2,128)S(1)}) fusion(f32[4,2,5120]{2,1,0:T(2,128)} %all-reduce.7.cloned.1.call-done, u32[]{:T(128)} %bitcast.11, f32[1,2,5120]{2,1,0:T(2,128)S(1)} %mul.71, bf16[1,2,5120]{2,1,0:T(2,128)(2,1)S(1)} %copy-done.2, ...), kind=kLoop, calls=%fused_computation.5 | loop fusion | flops 133120 | bytes 327684
  115.3 0.1 bitcast_reduce_fusion
  115.4 0.6 fusion.2
  116.0 0.1 div.51
  116.1 0.6 fusion.1
  116.7 0.1 div.48
  116.8 0.8 fusion.4
  117.6 13.2 %all_gather.6 = bf16[4,2,5120]{2,1,0:T(2,128)(2,1)S(1)} all-gather(bf16[1,2,5120]{2,1,0:T(2,128)(2,1)S(1)} %get-tuple-element.16), channel_id=1, replica_groups=mesh['gx'=8,'gy'=4] {'gy'}, dimensions={0}, use_global_device_ids=true | all-gather | bytes 102400 | tf_op jit(solution)/shard_map/all_gather | solution.py:60
  130.8 10.0 %all_gather.7 = bf16[32,2,5120]{2,1,0:T(2,128)(2,1)S(1)} all-gather(bf16[4,2,5120]{2,1,0:T(2,128)(2,1)S(1)} %all_gather.6), channel_id=1, replica_groups=mesh['gx'=8,'gy'=4] {'gx'}, dimensions={0}, use_global_device_ids=true | all-gather | bytes 737280 | tf_op jit(solution)/shard_map/all_gather | solution.py:61
  140.8 0.8 copy.32
  (19 shorter events, 0.2 us)
Async XLA Ops:
  7.2 0.9 copy-start
  7.2 9.2 %copy-start.7 = (u32[32]{0:T(128)S(1)}, u32[32]{0:T(128)}, u32[]{:S(2)}) copy-start(u32[32]{0:T(128)} %constant.29) | copy-start | bytes 388
  7.2 71.6 %copy-start.6 = (u32[32]{0:T(128)S(1)}, u32[32]{0:T(128)}, u32[]{:S(2)}) copy-start(u32[32]{0:T(128)} %constant.33) | copy-start | bytes 388
  7.2 72.2 %copy-start.4 = (f32[1,2,40]{2,1,0:T(2,128)S(1)}, f32[1,2,40]{2,1,0:T(2,128)}, u32[]{:S(2)}) copy-start(f32[1,2,40]{2,1,0:T(2,128)} %param.11) | copy-start | bytes 964
  7.2 72.3 %copy-start.5 = (f32[1,2,40]{2,1,0:T(2,128)S(1)}, f32[1,2,40]{2,1,0:T(2,128)}, u32[]{:S(2)}) copy-start(f32[1,2,40]{2,1,0:T(2,128)} %param.13) | copy-start | bytes 964
  7.2 106.6 %copy-start.2 = (bf16[1,2,5120]{2,1,0:T(2,128)(2,1)S(1)}, bf16[1,2,5120]{2,1,0:T(2,128)(2,1)}, u32[]{:S(2)}) copy-start(bf16[1,2,5120]{2,1,0:T(2,128)(2,1)} %param.10) | copy-start | bytes 61444
  7.2 106.6 %copy-start.3 = (bf16[1,2,5120]{2,1,0:T(2,128)(2,1)S(1)}, bf16[1,2,5120]{2,1,0:T(2,128)(2,1)}, u32[]{:S(2)}) copy-start(bf16[1,2,5120]{2,1,0:T(2,128)(2,1)} %param.12) | copy-start | bytes 61444
  7.2 109.5 %copy-start.1 = (f32[1,2,5120]{2,1,0:T(2,128)S(1)}, f32[1,2,5120]{2,1,0:T(2,128)}, u32[]{:S(2)}) copy-start(f32[1,2,5120]{2,1,0:T(2,128)} %param.9) | copy-start | bytes 122884
  7.3 69.7 %all-reduce.5.cloned.1.call-start = ((), (), s32[]{:S(2)}) async-start(), calls=%async_computation | async-start | bytes 2621440
  16.3 97.5 %all-reduce.7.cloned.1.call-start = ((), (), s32[]{:S(2)}) async-start(), calls=%async_computation.1 | async-start | bytes 327680
Sparse Core Ops, SparseCore 0:
  16.4 60.4 all-reduce.4
  79.8 33.9 all-reduce.6
where the time goes:
time: 149 us; the launch traced here: 148 us
  waiting for transfers between devices  93.6 us (63%)
  blocking collectives  23.2 us (16%)
  between operations  14.8 us (10%)
  matrix products  8.18 us (5%)
  local copies, waits for them, and re-layouts  5.03 us (3%)
  other arithmetic  3.53 us (2%)
    unnamed x4, waiting for transfers between devices  93.6 us
    all_gather x1, blocking collectives, body(): inner_weights = lax.all_gather(local_weights, 'gy', axis=0, tiled=True)  13.2 us
    all_gather x1, blocking collectives, body(): new_weights = lax.all_gather(inner_weights, 'gx', axis=0, tiled=True)  9.99 us
    unnamed x1, matrix products  8.18 us
    unnamed x20, local copies, waits for them, and re-layouts  3.84 us
  transfers between devices with their start and end apart: 2, of which 2 were waited for; matrix products, arithmetic and copies ran while one was open for 1% of the time, Pallas kernels for 0%

commit v1 on v0

v1 whole, which is shorter than its diff:
```python
import functools

import jax
import jax.numpy as jnp
import numpy as np
from jax import lax
from jax.experimental import pallas as pl
from jax.experimental.pallas import tpu as pltpu
from jax.sharding import PartitionSpec as P

beta_one = 0.9
beta_two = 0.95
epsilon = 1e-08
learn_rate = 0.01
decay_rate = 0.1
step_count = 10

MESH = pl.DeviceIdType.MESH
CHUNKS = 5


def chunk_widths(width_all, group):
    groups = width_all // group
    edges = [groups * i // CHUNKS for i in range(CHUNKS + 1)]
    return [(b - a) * group for a, b in zip(edges, edges[1:])]


def stage_order(count):
    gaps = [0.0, 2.0, 4.0, 3.5, 3.0, 3.5, 1.5]
    items = []
    for c in range(count):
        t = 3.0 + 1.3 * c
        for s, gap in enumerate(gaps):
            t += gap
            items.append((t, s, c))
    return [(s, c) for _, s, c in sorted(items)]


def kernel(nx, ny, widths, group, *refs):
    (act_hbm, og_ref, perm_ref, master_ref, first_ref, fscale_ref, second_ref, sscale_ref,
     w_out, master_out, first_out, fscale_out, second_out, sscale_out) = refs[:14]
    refs = refs[14:]
    n = len(widths)
    lhs, refs = refs[0], refs[1:]
    act, part, rx1, rx2, s2, rx3 = (refs[i * n:(i + 1) * n] for i in range(6))
    (act_sem, p_send, p_recv, q_send, q_recv, g_send, g_recv,
     ag_send, ag_recv, aq_send, aq_recv, ap_send, ap_recv) = refs[6 * n:]
    starts = [sum(widths[:c]) for c in range(n)]

    gx, gy = lax.axis_index("gx"), lax.axis_index("gy")
    nq = nx // 2
    core, quad = lax.rem(gx, 2), gx // 2
    other = 1 - core
    partner = (quad * 2 + other, gy)

    def quad_at(j):
        return lax.rem(quad + j, nq)

    def quad_dev(j):
        return (quad_at(j) * 2 + core, gy)

    def gy_at(j):
        return lax.rem(gy + j, ny)

    def fetch(c):
        return pltpu.make_async_copy(
            act_hbm.at[:, pl.ds(starts[c], widths[c])], act[c], act_sem.at[c])

    for c in range(n):
        fetch(c).start()

    barrier = pltpu.get_barrier_semaphore()
    pl.semaphore_signal(barrier, inc=1, device_id=partner, device_id_type=MESH)
    for j in range(1, nq):
        pl.semaphore_signal(barrier, inc=1, device_id=quad_dev(j), device_id_type=MESH)
    for j in range(1, ny):
        pl.semaphore_signal(barrier, inc=1, device_id=(gx, gy_at(j)), device_id_type=MESH)

    nt = (((1,), (1,)), ((), ()))
    lhs[...] = (
        lax.dot_general(perm_ref[0], og_ref[0], nt, preferred_element_type=jnp.float32)
        + lax.dot_general(perm_ref[1], og_ref[1], nt, preferred_element_type=jnp.float32)
    ).astype(jnp.bfloat16)

    pl.semaphore_wait(barrier, nq + ny - 1)

    def remote(src, dst, send, recv, device):
        return pltpu.make_async_remote_copy(
            src_ref=src, dst_ref=dst, send_sem=send, recv_sem=recv,
            device_id=device, device_id_type=MESH)

    def pair_copy(c):
        return remote(part[c].at[other], rx1[c], p_send.at[c], p_recv.at[c], partner)

    def quad_copy(c, j):
        return remote(part[c].at[core, quad_at(j)], rx2[c].at[j - 1],
                      q_send.at[c, j - 1], q_recv.at[c, j - 1], quad_dev(j))

    def gy_copy(c, j):
        return remote(s2[c].at[gy_at(j)], rx3[c].at[j - 1],
                      g_send.at[c, j - 1], g_recv.at[c, j - 1], (gx, gy_at(j)))

    def rows_of(c, first, count):
        ref = w_out.at[pl.ds(first, count), :, pl.ds(starts[c], widths[c])]
        return ref

    def ag_copy(c, j):
        ref = rows_of(c, gx * ny + gy, 1)
        return remote(ref, ref, ag_send.at[c, j - 1], ag_recv.at[c, j - 1], (gx, gy_at(j)))

    def aq_copy(c, j):
        ref = rows_of(c, gx * ny, ny)
        return remote(ref, ref, aq_send.at[c, j - 1], aq_recv.at[c, j - 1], quad_dev(j))

    def ap_copy(c, j):
        ref = rows_of(c, (quad_at(nq - j) * 2 + core) * ny, ny)
        return remote(ref, ref, ap_send.at[c, j], ap_recv.at[c, j], partner)

    def adam(c, grad):
        gpc = widths[c] // group
        g0 = starts[c] // group
        lane = lax.broadcasted_iota(jnp.int32, (2, fscale_ref.shape[2]), 1)
        fs_all, ss_all = fscale_out[0], sscale_out[0]
        for i in range(gpc):
            cols = pl.ds(starts[c] + i * group, group)
            g = grad[:, i * group:(i + 1) * group]
            fs = fscale_ref[0, :, pl.ds(g0 + i, 1)]
            ss = sscale_ref[0, :, pl.ds(g0 + i, 1)]
            master = master_ref[0, :, cols]
            m_old = first_ref[0, :, cols].astype(jnp.float32) * fs
            v_old = second_ref[0, :, cols].astype(jnp.float32) * ss
            m = beta_one * m_old + (1.0 - beta_one) * g
            v = beta_two * v_old + (1.0 - beta_two) * g * g
            update = m / (1.0 - beta_one**step_count) / (
                jnp.sqrt(v / (1.0 - beta_two**step_count)) + epsilon)
            new = master - learn_rate * (update + decay_rate * master)
            master_out[0, :, cols] = new
            w_out[pl.ds(gx * ny + gy, 1), :, cols] = new.astype(jnp.bfloat16)[None]
            nfs = jnp.max(jnp.abs(m), axis=1, keepdims=True) + 1e-06
            nss = jnp.max(jnp.abs(v), axis=1, keepdims=True) + 1e-06
            first_out[0, :, cols] = (m / nfs).astype(jnp.bfloat16)
            second_out[0, :, cols] = (v / nss).astype(jnp.bfloat16)
            fs_all = jnp.where(lane == g0 + i, nfs, fs_all)
            ss_all = jnp.where(lane == g0 + i, nss, ss_all)
        fscale_out[0], sscale_out[0] = fs_all, ss_all

    fscale_out[...] = jnp.zeros_like(fscale_out)
    sscale_out[...] = jnp.zeros_like(sscale_out)

    for stage, c in stage_order(n):
        if stage == 0:
            fetch(c).wait()
            res = jnp.dot(lhs[...], act[c][...], preferred_element_type=jnp.float32)
            part[c][...] = res.reshape(part[c].shape)
            pair_copy(c).start()
        elif stage == 1:
            pair_copy(c).wait_recv()
            for j in list(range(1, nq)) + [nq]:
                at = quad_at(j)
                part[c][core, at] = part[c][core, at] + rx1[c][at]
                if j < nq:
                    quad_copy(c, j).start()
        elif stage == 2:
            total = part[c][core, quad]
            for j in range(1, nq):
                quad_copy(c, j).wait_recv()
                total = total + rx2[c][j - 1]
            for g in range(ny):
                s2[c][g] = total[2 * g:2 * g + 2]
            for j in range(1, ny):
                gy_copy(c, j).start()
        elif stage == 3:
            grad = s2[c][gy]
            for j in range(1, ny):
                gy_copy(c, j).wait_recv()
                grad = grad + rx3[c][j - 1]
            adam(c, grad)
            for j in range(1, ny):
                ag_copy(c, j).start()
        elif stage == 4:
            for j in range(1, ny):
                ag_copy(c, j).wait_recv()
            for j in range(1, nq):
                aq_copy(c, j).start()
            ap_copy(c, 0).start()
        elif stage == 5:
            for j in range(1, nq):
                aq_copy(c, j).wait_recv()
                ap_copy(c, j).start()
        else:
            for j in range(nq):
                ap_copy(c, j).wait_recv()

    for c in range(n):
        pair_copy(c).wait_send()
        for j in range(1, nq):
            quad_copy(c, j).wait_send()
            aq_copy(c, j).wait_send()
        for j in range(1, ny):
            gy_copy(c, j).wait_send()
            ag_copy(c, j).wait_send()
        for j in range(nq):
            ap_copy(c, j).wait_send()


def body(nx, ny, activations, out_grad, master, first_moment, first_scale, second_moment, second_scale):
    tokens, width_all = activations.shape
    rows = out_grad.shape[2]
    group = width_all // first_scale.shape[2]
    widths = chunk_widths(width_all, group)
    n = len(widths)
    nq = nx // 2
    assert rows == nx * ny and nx % 2 == 0

    perm = np.zeros((2, 2 * rows, rows), np.float32)
    spot = 0
    for core in range(2):
        for quad in range(nq):
            for g in range(ny):
                for p in range(2):
                    perm[p, spot, (quad * 2 + core) * ny + g] = 1.0
                    spot += 1
    perm = jnp.asarray(perm, jnp.bfloat16)

    vmem = pl.BlockSpec(memory_space=pltpu.VMEM)
    f32, bf16 = jnp.float32, jnp.bfloat16
    dma = pltpu.SemaphoreType.DMA
    scratch = [pltpu.VMEM((2 * rows, tokens), bf16)]
    scratch += [pltpu.VMEM((tokens, w), bf16) for w in widths]
    scratch += [pltpu.VMEM((2, nq, 2 * ny, w), f32) for w in widths]
    scratch += [pltpu.VMEM((nq, 2 * ny, w), f32) for w in widths]
    scratch += [pltpu.VMEM((nq - 1, 2 * ny, w), f32) for w in widths]
    scratch += [pltpu.VMEM((ny, 2, w), f32) for w in widths]
    scratch += [pltpu.VMEM((ny - 1, 2, w), f32) for w in widths]
    scratch += [dma((n,)), dma((n,)), dma((n,))]
    scratch += [dma((n, nq - 1)), dma((n, nq - 1)), dma((n, ny - 1)), dma((n, ny - 1))]
    scratch += [dma((n, ny - 1)), dma((n, ny - 1)), dma((n, nq - 1)), dma((n, nq - 1))]
    scratch += [dma((n, nq)), dma((n, nq))]
    shape = jax.ShapeDtypeStruct
    return pl.pallas_call(
        functools.partial(kernel, nx, ny, widths, group),
        out_shape=(
            shape((rows, 2, width_all), bf16),
            shape(master.shape, f32),
            shape(first_moment.shape, bf16),
            shape(first_scale.shape, f32),
            shape(second_moment.shape, bf16),
            shape(second_scale.shape, f32),
        ),
        in_specs=[pl.BlockSpec(memory_space=pl.ANY)] + [vmem] * 7,
        out_specs=[vmem] * 6,
        scratch_shapes=scratch,
        compiler_params=pltpu.CompilerParams(
            collective_id=0, has_side_effects=True, vmem_limit_bytes=60 * 1024 * 1024),
    )(activations, out_grad, perm, master, first_moment, first_scale, second_moment, second_scale)


def solution(mesh):
    nx, ny = mesh.shape["gx"], mesh.shape["gy"]
    rows = P(("gx", "gy"), None, None)
    in_specs = (P(("gx", "gy"), None), P(None, ("gx", "gy"), None), rows, rows, rows, rows, rows)
    out_specs = (P(), rows, rows, rows, rows, rows)
    return jax.shard_map(
        functools.partial(body, nx, ny), mesh=mesh, in_specs=in_specs, out_specs=out_specs,
        check_vma=False)
```

time: 149 us -> 43.8 us (0.29)
  waiting for transfers between devices: 93.6 us -> 0 us
  Pallas kernels: 0 us -> 31.8 us
  blocking collectives: 23.2 us -> 0 us
  between operations: 14.8 us -> 0.64 us
  matrix products: 8.18 us -> 0 us
  local copies, waits for them, and re-layouts: 5.03 us -> 10.9 us
  other arithmetic: 3.53 us -> 0 us
    unnamed x4 -> x0, waiting for transfers between devices: 93.6 us -> none
    pallas_call x0 -> x1, Pallas kernels: none -> 31.8 us  [body(): pl.pallas_call(functools.partial(kernel, nx, ny, widths, group), out_shap...]
    all_gather x2 -> x0, blocking collectives: 23.2 us -> none  [the longest x1 13.2 us: body(): inner_weights = lax.all_gather(local_weights, 'gy', axis=0, tiled=True)]
    unnamed x1 -> x0, matrix products: 8.18 us -> none
    unnamed x20 -> x7, local copies, waits for them, and re-layouts: 3.84 us -> 10.9 us
    unnamed x1 -> x0, other arithmetic: 1.53 us -> none
  transfers between devices with their start and end apart: 2 -> 0, of which waited for: 2 -> 0; matrix products, arithmetic and copies ran while one was open for 1% -> 0% of each run, Pallas kernels for 0% -> 0%
where the time goes in v1:
time: 43.8 us; the launch traced here: 43.4 us
  Pallas kernels  31.8 us (73%)
  local copies, waits for them, and re-layouts  10.9 us (25%)
  between operations  0.64 us (1%)
    pallas_call x1, Pallas kernels, body(): pl.pallas_call(functools.partial(kernel, nx, ny, widths, group), out_shap...  31.8 us
    unnamed x7, local copies, waits for them, and re-layouts  10.9 us

profile of v1, /device:TPU:0, one launch (start us, length us, event | category | flops | bytes accessed | tf_op | source)
XLA Modules:
  0.0 43.4 jit_solution(15348862946663257587)
XLA Ops:
  0.6 2.0 %copy.14.refs_1_ = bf16[2,1280,32]{2,1,0:T(8,128)(2,1)} copy(bf16[2,1280,32]{1,2,0:T(8,128)(2,1)} %param.9) | data formatting | bytes 327680 | tf_op args[1]
  2.6 31.8 %shard_map.127 = (bf16[32,2,5120]{2,1,0:T(2,128)(2,1)}, f32[1,2,5120]{2,1,0:T(2,128)}, bf16[1,2,5120]{2,1,0:T(2,128)(2,1)}, f32[1,2,40]{2,1,0:T(2,128)}, bf16[1,...) custom-call(bf16[1280,5120]{1,0:T(8,128)(2,1)} %refs_0_.1, bf16[2,1280,32]{2,1,0:T(8,128)(2,1)} %copy.14.refs_1_, ...), custom_call_target="tpu_custom_call" | custom-call | tf_op jit(solution)/shard_map/pallas_call | solution.py:240
  34.4 2.4 %copy.21 = bf16[32,2,5120]{2,1,0:T(2,128)(2,1)} copy(bf16[32,2,5120]{2,1,0:T(2,128)(2,1)} %get-tuple-element.12) | data formatting | bytes 1310720
  36.8 1.4 %copy.22 = f32[1,2,5120]{2,1,0:T(2,128)} copy(f32[1,2,5120]{2,1,0:T(2,128)} %get-tuple-element.13) | data formatting | bytes 81920
  38.2 1.3 %copy.23 = bf16[1,2,5120]{2,1,0:T(2,128)(2,1)} copy(bf16[1,2,5120]{2,1,0:T(2,128)(2,1)} %get-tuple-element.14) | data formatting | bytes 40960
  39.6 1.2 %copy.24 = f32[1,2,40]{2,1,0:T(2,128)} copy(f32[1,2,40]{2,1,0:T(2,128)} %get-tuple-element.15) | data formatting | bytes 640
  40.8 1.3 %copy.25 = bf16[1,2,5120]{2,1,0:T(2,128)(2,1)} copy(bf16[1,2,5120]{2,1,0:T(2,128)(2,1)} %get-tuple-element.16) | data formatting | bytes 40960
  42.1 1.2 %copy.26 = f32[1,2,40]{2,1,0:T(2,128)} copy(f32[1,2,40]{2,1,0:T(2,128)} %get-tuple-element.17) | data formatting | bytes 640

commit v2 on v1

--- a/solution.py
+++ b/solution.py
@@ -37,9 +37,12 @@
 
 
 def kernel(nx, ny, widths, group, *refs):
-    (act_hbm, og_ref, perm_ref, master_ref, first_ref, fscale_ref, second_ref, sscale_ref,
-     w_out, master_out, first_out, fscale_out, second_out, sscale_out) = refs[:14]
-    refs = refs[14:]
+    act_hbm, held = refs[0], refs[1:8]
+    w_out, master_out, first_out, fscale_out, second_out, sscale_out = refs[8:14]
+    local = refs[14:21]
+    og_ref, perm_ref, master_ref, first_ref, fscale_ref, second_ref, sscale_ref = local
+    in_sem = refs[21]
+    refs = refs[22:]
     n = len(widths)
     lhs, refs = refs[0], refs[1:]
     act, part, rx1, rx2, s2, rx3 = (refs[i * n:(i + 1) * n] for i in range(6))
@@ -66,8 +69,15 @@
         return pltpu.make_async_copy(
             act_hbm.at[:, pl.ds(starts[c], widths[c])], act[c], act_sem.at[c])
 
-    for c in range(n):
+    def take(i):
+        return pltpu.make_async_copy(held[i], local[i], in_sem.at[i])
+
+    take(0).start()
+    take(1).start()
+    for c in range(min(2, n)):
         fetch(c).start()
+    for i in range(2, 7):
+        take(i).start()
 
     barrier = pltpu.get_barrier_semaphore()
     pl.semaphore_signal(barrier, inc=1, device_id=partner, device_id_type=MESH)
@@ -76,10 +86,11 @@
     for j in range(1, ny):
         pl.semaphore_signal(barrier, inc=1, device_id=(gx, gy_at(j)), device_id_type=MESH)
 
-    nt = (((1,), (1,)), ((), ()))
+    take(0).wait()
+    take(1).wait()
     lhs[...] = (
-        lax.dot_general(perm_ref[0], og_ref[0], nt, preferred_element_type=jnp.float32)
-        + lax.dot_general(perm_ref[1], og_ref[1], nt, preferred_element_type=jnp.float32)
+        jnp.dot(perm_ref[0], og_ref[0], preferred_element_type=jnp.float32)
+        + jnp.dot(perm_ref[1], og_ref[1], preferred_element_type=jnp.float32)
     ).astype(jnp.bfloat16)
 
     pl.semaphore_wait(barrier, nq + ny - 1)
@@ -117,11 +128,9 @@
         return remote(ref, ref, ap_send.at[c, j], ap_recv.at[c, j], partner)
 
     def adam(c, grad):
-        gpc = widths[c] // group
+        moments = []
         g0 = starts[c] // group
-        lane = lax.broadcasted_iota(jnp.int32, (2, fscale_ref.shape[2]), 1)
-        fs_all, ss_all = fscale_out[0], sscale_out[0]
-        for i in range(gpc):
+        for i in range(widths[c] // group):
             cols = pl.ds(starts[c] + i * group, group)
             g = grad[:, i * group:(i + 1) * group]
             fs = fscale_ref[0, :, pl.ds(g0 + i, 1)]
@@ -136,6 +145,15 @@
             new = master - learn_rate * (update + decay_rate * master)
             master_out[0, :, cols] = new
             w_out[pl.ds(gx * ny + gy, 1), :, cols] = new.astype(jnp.bfloat16)[None]
+            moments.append((m, v))
+        return moments
+
+    def requant(c, moments):
+        g0 = starts[c] // group
+        lane = lax.broadcasted_iota(jnp.int32, (2, fscale_ref.shape[2]), 1)
+        fs_all, ss_all = fscale_out[0], sscale_out[0]
+        for i, (m, v) in enumerate(moments):
+            cols = pl.ds(starts[c] + i * group, group)
             nfs = jnp.max(jnp.abs(m), axis=1, keepdims=True) + 1e-06
             nss = jnp.max(jnp.abs(v), axis=1, keepdims=True) + 1e-06
             first_out[0, :, cols] = (m / nfs).astype(jnp.bfloat16)
@@ -147,9 +165,12 @@
     fscale_out[...] = jnp.zeros_like(fscale_out)
     sscale_out[...] = jnp.zeros_like(sscale_out)
 
+    taken = []
     for stage, c in stage_order(n):
         if stage == 0:
             fetch(c).wait()
+            if c + 2 < n:
+                fetch(c + 2).start()
             res = jnp.dot(lhs[...], act[c][...], preferred_element_type=jnp.float32)
             part[c][...] = res.reshape(part[c].shape)
             pair_copy(c).start()
@@ -174,9 +195,14 @@
             for j in range(1, ny):
                 gy_copy(c, j).wait_recv()
                 grad = grad + rx3[c][j - 1]
-            adam(c, grad)
+            if not taken:
+                for i in range(2, 7):
+                    take(i).wait()
+                taken.append(True)
+            moments = adam(c, grad)
             for j in range(1, ny):
                 ag_copy(c, j).start()
+            requant(c, moments)
         elif stage == 4:
             for j in range(1, ny):
                 ag_copy(c, j).wait_recv()
@@ -203,6 +229,17 @@
             ap_copy(c, j).wait_send()
 
 
+def spill(*refs):
+    count = (len(refs) - 1) // 2
+    sem = refs[-1]
+    copies = [
+        pltpu.make_async_copy(refs[i], refs[count + i], sem.at[i]) for i in range(count)]
+    for copy in copies:
+        copy.start()
+    for copy in copies:
+        copy.wait()
+
+
 def body(nx, ny, activations, out_grad, master, first_moment, first_scale, second_moment, second_scale):
     tokens, width_all = activations.shape
     rows = out_grad.shape[2]
@@ -225,7 +262,10 @@
     vmem = pl.BlockSpec(memory_space=pltpu.VMEM)
     f32, bf16 = jnp.float32, jnp.bfloat16
     dma = pltpu.SemaphoreType.DMA
-    scratch = [pltpu.VMEM((2 * rows, tokens), bf16)]
+    grads = jnp.swapaxes(out_grad, 1, 2)
+    small = (grads, perm, master, first_moment, first_scale, second_moment, second_scale)
+    scratch = [pltpu.VMEM(x.shape, x.dtype) for x in small] + [dma((len(small),))]
+    scratch += [pltpu.VMEM((2 * rows, tokens), bf16)]
     scratch += [pltpu.VMEM((tokens, w), bf16) for w in widths]
     scratch += [pltpu.VMEM((2, nq, 2 * ny, w), f32) for w in widths]
     scratch += [pltpu.VMEM((nq, 2 * ny, w), f32) for w in widths]
@@ -236,8 +276,11 @@
     scratch += [dma((n, nq - 1)), dma((n, nq - 1)), dma((n, ny - 1)), dma((n, ny - 1))]
     scratch += [dma((n, ny - 1)), dma((n, ny - 1)), dma((n, nq - 1)), dma((n, nq - 1))]
     scratch += [dma((n, nq)), dma((n, nq))]
+    held = sum(
+        int(np.prod(x.shape)) * jnp.dtype(x.dtype).itemsize
+        for x in scratch if x.memory_space == pltpu.VMEM)
     shape = jax.ShapeDtypeStruct
-    return pl.pallas_call(
+    outs = pl.pallas_call(
         functools.partial(kernel, nx, ny, widths, group),
         out_shape=(
             shape((rows, 2, width_all), bf16),
@@ -247,12 +290,20 @@
             shape(second_moment.shape, bf16),
             shape(second_scale.shape, f32),
         ),
-        in_specs=[pl.BlockSpec(memory_space=pl.ANY)] + [vmem] * 7,
+        in_specs=[pl.BlockSpec(memory_space=pltpu.HBM)] * 8,
         out_specs=[vmem] * 6,
         scratch_shapes=scratch,
         compiler_params=pltpu.CompilerParams(
-            collective_id=0, has_side_effects=True, vmem_limit_bytes=60 * 1024 * 1024),
-    )(activations, out_grad, perm, master, first_moment, first_scale, second_moment, second_scale)
+            collective_id=0, has_side_effects=True, vmem_limit_bytes=min(held + held // 8 + 4 * 1024 * 1024, 60 * 1024 * 1024)),
+    )(*(pltpu.with_memory_space_constraint(x, pltpu.HBM) for x in (activations, *small)))
+    return pl.pallas_call(
+        spill,
+        out_shape=tuple(shape(out.shape, out.dtype) for out in outs),
+        in_specs=[vmem] * 6,
+        out_specs=[pl.BlockSpec(memory_space=pltpu.HBM)] * 6,
+        scratch_shapes=[dma((6,))],
+        compiler_params=pltpu.CompilerParams(vmem_limit_bytes=1024 * 1024),
+    )(*outs)
 
 
 def solution(mesh):

time: 43.8 us -> 31.3 us (0.71)
  local copies, waits for them, and re-layouts: 10.9 us -> 0 us
  Pallas kernels: 31.8 us -> 30.5 us
    unnamed x7 -> x0, local copies, waits for them, and re-layouts: 10.9 us -> none
    pallas_call x1, Pallas kernels: 31.8 us -> 29.6 us  [body(): pl.pallas_call(functools.partial(kernel, nx, ny, widths, group), out_shap...]
    pallas_call x0 -> x1, Pallas kernels: none -> 0.9 us  [body(): pl.pallas_call(spill, out_shape=tuple((shape(out.shape, out.dtype) for ou...]
where the time goes in v2:
time: 31.3 us; the launch traced here: 31.1 us
  Pallas kernels  30.5 us (97%)
  between operations  0.64 us (2%)
    pallas_call x1, Pallas kernels, body(): pl.pallas_call(functools.partial(kernel, nx, ny, widths, group), out_shap...  29.6 us
    pallas_call x1, Pallas kernels, body(): pl.pallas_call(spill, out_shape=tuple((shape(out.shape, out.dtype) for ou...  0.9 us

profile of v2, /device:TPU:0, one launch (start us, length us, event | category | flops | bytes accessed | tf_op | source)
XLA Modules:
  0.0 31.1 jit_solution(7675069746722836707)
XLA Ops:
  0.6 29.6 %shard_map.127 = (bf16[32,2,5120]{2,1,0:T(2,128)(2,1)S(1)}, f32[1,2,5120]{2,1,0:T(2,128)S(1)}, bf16[1,2,5120]{2,1,0:T(2,128)(2,1)S(1)}, f32[1,2,40]{2,1,0:T(2,12...) custom-call(bf16[1280,5120]{1,0:T(8,128)(2,1)} %refs_0_.1, bf16[2,32,1280]{2,1,0:T(8,128)(2,1)} %bitcast.1, ...), custom_call_target="tpu_custom_call" | custom-call | tf_op jit(solution)/shard_map/pallas_call | solution.py:283
  30.2 0.9 %shard_map.128 = (bf16[32,2,5120]{2,1,0:T(2,128)(2,1)}, f32[1,2,5120]{2,1,0:T(2,128)}, bf16[1,2,5120]{2,1,0:T(2,128)(2,1)}, f32[1,2,40]{2,1,0:T(2,128)}, bf16[1,...) custom-call(bf16[32,2,5120]{2,1,0:T(2,128)(2,1)S(1)} %get-tuple-element.12.refs_0_, ...), custom_call_target="tpu_custom_call" | custom-call | tf_op jit(solution)/shard_map/pallas_call | solution.py:299
